TPU v7x, 512 devices: a whole 4x8x8 slice. The times are simulated.
512 devices in a mesh: rows: 128 (over z, y, x_lo), feat: 4 (over x_hi, core).
Axes of the slice: x: 4 (x_hi: 2, x_lo: 2; x = x_hi * 2 + x_lo), y: 8, z: 8, core: 2. Of those that a mesh axis runs over, the one named last changes fastest.
Arguments:
- bin_index: int32 [262144, 512], P('rows', 'feat'), may hold values from 0 to 255
- leaf_ids: int32 [262144], P('rows'), may hold values from 0 to 15
- gradients: bfloat16 [262144], P('rows'), may hold values from -3 to 3
- hessians: bfloat16 [262144], P('rows'), may hold values from 0.049804688 to 0.25
Outputs:
- split_gains: float32 [4, 128, 16, 256], P('feat', 'rows')
- best_gain: float32 [16], replicated
All inputs are finite; a program needn't handle non-finite values.
Results may differ from a plain program's by a relative error of at most 0.0003.
Values may be sent and summed in bfloat16 or wider, within the bound.
A program may use at most 64 MiB of HBM per device.

v0:
```python
import functools
import math

import jax
import jax.numpy as jnp
from jax import lax
from jax.sharding import Mesh
from jax.sharding import PartitionSpec as P

BINS = 256
LEAVES = 16
ROWS = ("rows_0", "rows_1", "rows_2")
ROWS_FEAT = ("rows_0", "rows_1", "rows_2", "feat_0", "feat_1")
FEAT = ("feat_0", "feat_1")


reg_lambda = 1.0


def own_rows(total, axes):
    for axis in axes:
        total = lax.psum_scatter(total, axis, scatter_dimension=0, tiled=True)
    return total


def one_axis_at_a_time(array, axes):
    return functools.reduce(lax.pmax, axes, array)


def gain_of(left_grad, left_hess):
    total_grad = left_grad[:, :, -1:]
    total_hess = left_hess[:, :, -1:]
    right_grad = total_grad - left_grad
    right_hess = total_hess - left_hess
    return 0.5 * (
        left_grad * left_grad / (left_hess + reg_lambda)
        + right_grad * right_grad / (right_hess + reg_lambda)
        - total_grad * total_grad / (total_hess + reg_lambda)
    )


def leaf_table(leaf_ids, gradients, hessians):
    members = leaf_ids[None, :] == jnp.arange(LEAVES, dtype=jnp.int32)[:, None]
    zero_value = jnp.zeros((), jnp.bfloat16)
    grad_part = jnp.where(members, gradients[None, :], zero_value)
    hess_part = jnp.where(members, hessians[None, :], zero_value)
    return jnp.concatenate([grad_part, hess_part], axis=0)


def partial_hist(weights, columns):
    onehot = (columns[:, :, None] == jnp.arange(BINS, dtype=jnp.int32)).astype(jnp.bfloat16)
    return jnp.einsum("cr,rfb->fcb", weights, onehot, preferred_element_type=jnp.float32)


def body(bin_index, leaf_ids, gradients, hessians):
    local_features = bin_index.shape[1]
    own_columns = local_features // lax.axis_size(ROWS)
    weights = leaf_table(leaf_ids, gradients, hessians)
    group_width = math.gcd(own_columns * lax.axis_size(ROWS), 8)
    group_count = own_columns * lax.axis_size(ROWS) // group_width

    def one_group(position):
        part_columns = lax.dynamic_slice_in_dim(bin_index, position * group_width, group_width, 1)
        return partial_hist(weights, part_columns)

    stacked = lax.map(one_group, jnp.arange(group_count, dtype=jnp.int32))
    totals = own_rows(stacked.reshape(own_columns * lax.axis_size(ROWS), 2 * LEAVES, BINS), ROWS)
    left_sums = jnp.cumsum(totals, axis=2)
    split_gains = gain_of(left_sums[:, :LEAVES], left_sums[:, LEAVES:])
    best_gain = one_axis_at_a_time(jnp.max(split_gains, axis=(0, 2)), ROWS_FEAT)
    return (split_gains[None], best_gain)


def solution(mesh):
    torus = Mesh(
        mesh.devices.reshape(8, 8, 2, 2, 2), ("rows_0", "rows_1", "rows_2", "feat_0", "feat_1")
    )
    return jax.shard_map(
        body,
        mesh=torus,
        in_specs=(P(ROWS, FEAT), P(ROWS), P(ROWS), P(ROWS)),
        out_specs=(P(FEAT, ROWS, None, None), P()),
        check_vma=False,
    )
```

profile of v0, /device:TPU:1, one launch (start us, length us, event | category | flops | bytes accessed | tf_op | source)
XLA Modules:
  0.0 294.1 jit_solution(17963851640945320323)
XLA Ops:
  7.2 1.6 copy.19
  8.8 0.7 fusion.6
  9.6 100.4 %while.10 = (s32[]{:T(128)}, f32[16,8,32,256]{3,2,1,0:T(8,128)}, s32[16]{0:T(128)S(1)}, s32[2048,128]{0,1:T(8,128)S(1)}, bf16[32,2048]{1,0:T(8,128)(2,1)S(1)}, /...) while((s32[]{:T(128)}, f32[16,8,32,256]{3,2,1,0:T(8,128)}, s32[16]{0:T(128)S(1)}, ...), condition=%wide.region_1.2_spmd, body=%wide.region_0.1_spmd.sunk | while | flops 272629760 | bytes 590491 | solution.py:66
  9.6 0.6 dynamic_slice.11
  10.8 5.0 %fusion.12 = f32[16,8,32,256]{3,2,1,0:T(8,128)} fusion(f32[16,8,32,256]{3,2,1,0:T(8,128)} %get-tuple-element.112, s32[]{:T(128)} %get-tuple-element.111, s32[2048,8]{0,1:T(8,128)S(1)} %constant_dynamic-slice_fusion.2, bf16[32,2048]{1,0:T(8,128)(2,1)S(1)} %get-tuple-element.124), kind=kOutput, calls=%fused_computation.4.clone.1 | convolution fusion | flops 272629760 | bytes 459264 | tf_op jit(solution)/shard_map/while/body/eval_jaxpr/cr,rfb->fcb/dot_general | solution.py:52
  17.1 5.0 %fusion.12 = f32[16,8,32,256]{3,2,1,0:T(8,128)} fusion(f32[16,8,32,256]{3,2,1,0:T(8,128)} %get-tuple-element.112, s32[]{:T(128)} %get-tuple-element.111, s32[2048,8]{0,1:T(8,128)S(1)} %constant_dynamic-slice_fusion.2, bf16[32,2048]{1,0:T(8,128)(2,1)S(1)} %get-tuple-element.124), kind=kOutput, calls=%fused_computation.4.clone.1 | convolution fusion | flops 272629760 | bytes 459264 | tf_op jit(solution)/shard_map/while/body/eval_jaxpr/cr,rfb->fcb/dot_general | solution.py:52
  23.4 5.0 %fusion.12 = f32[16,8,32,256]{3,2,1,0:T(8,128)} fusion(f32[16,8,32,256]{3,2,1,0:T(8,128)} %get-tuple-element.112, s32[]{:T(128)} %get-tuple-element.111, s32[2048,8]{0,1:T(8,128)S(1)} %constant_dynamic-slice_fusion.2, bf16[32,2048]{1,0:T(8,128)(2,1)S(1)} %get-tuple-element.124), kind=kOutput, calls=%fused_computation.4.clone.1 | convolution fusion | flops 272629760 | bytes 459264 | tf_op jit(solution)/shard_map/while/body/eval_jaxpr/cr,rfb->fcb/dot_general | solution.py:52
  29.7 5.0 %fusion.12 = f32[16,8,32,256]{3,2,1,0:T(8,128)} fusion(f32[16,8,32,256]{3,2,1,0:T(8,128)} %get-tuple-element.112, s32[]{:T(128)} %get-tuple-element.111, s32[2048,8]{0,1:T(8,128)S(1)} %constant_dynamic-slice_fusion.2, bf16[32,2048]{1,0:T(8,128)(2,1)S(1)} %get-tuple-element.124), kind=kOutput, calls=%fused_computation.4.clone.1 | convolution fusion | flops 272629760 | bytes 459264 | tf_op jit(solution)/shard_map/while/body/eval_jaxpr/cr,rfb->fcb/dot_general | solution.py:52
  35.9 5.0 %fusion.12 = f32[16,8,32,256]{3,2,1,0:T(8,128)} fusion(f32[16,8,32,256]{3,2,1,0:T(8,128)} %get-tuple-element.112, s32[]{:T(128)} %get-tuple-element.111, s32[2048,8]{0,1:T(8,128)S(1)} %constant_dynamic-slice_fusion.2, bf16[32,2048]{1,0:T(8,128)(2,1)S(1)} %get-tuple-element.124), kind=kOutput, calls=%fused_computation.4.clone.1 | convolution fusion | flops 272629760 | bytes 459264 | tf_op jit(solution)/shard_map/while/body/eval_jaxpr/cr,rfb->fcb/dot_general | solution.py:52
  42.2 5.0 %fusion.12 = f32[16,8,32,256]{3,2,1,0:T(8,128)} fusion(f32[16,8,32,256]{3,2,1,0:T(8,128)} %get-tuple-element.112, s32[]{:T(128)} %get-tuple-element.111, s32[2048,8]{0,1:T(8,128)S(1)} %constant_dynamic-slice_fusion.2, bf16[32,2048]{1,0:T(8,128)(2,1)S(1)} %get-tuple-element.124), kind=kOutput, calls=%fused_computation.4.clone.1 | convolution fusion | flops 272629760 | bytes 459264 | tf_op jit(solution)/shard_map/while/body/eval_jaxpr/cr,rfb->fcb/dot_general | solution.py:52
  48.5 5.0 %fusion.12 = f32[16,8,32,256]{3,2,1,0:T(8,128)} fusion(f32[16,8,32,256]{3,2,1,0:T(8,128)} %get-tuple-element.112, s32[]{:T(128)} %get-tuple-element.111, s32[2048,8]{0,1:T(8,128)S(1)} %constant_dynamic-slice_fusion.2, bf16[32,2048]{1,0:T(8,128)(2,1)S(1)} %get-tuple-element.124), kind=kOutput, calls=%fused_computation.4.clone.1 | convolution fusion | flops 272629760 | bytes 459264 | tf_op jit(solution)/shard_map/while/body/eval_jaxpr/cr,rfb->fcb/dot_general | solution.py:52
  53.5 0.6 dynamic_slice.11
  54.8 5.0 %fusion.12 = f32[16,8,32,256]{3,2,1,0:T(8,128)} fusion(f32[16,8,32,256]{3,2,1,0:T(8,128)} %get-tuple-element.112, s32[]{:T(128)} %get-tuple-element.111, s32[2048,8]{0,1:T(8,128)S(1)} %constant_dynamic-slice_fusion.2, bf16[32,2048]{1,0:T(8,128)(2,1)S(1)} %get-tuple-element.124), kind=kOutput, calls=%fused_computation.4.clone.1 | convolution fusion | flops 272629760 | bytes 459264 | tf_op jit(solution)/shard_map/while/body/eval_jaxpr/cr,rfb->fcb/dot_general | solution.py:52
  61.0 5.0 %fusion.12 = f32[16,8,32,256]{3,2,1,0:T(8,128)} fusion(f32[16,8,32,256]{3,2,1,0:T(8,128)} %get-tuple-element.112, s32[]{:T(128)} %get-tuple-element.111, s32[2048,8]{0,1:T(8,128)S(1)} %constant_dynamic-slice_fusion.2, bf16[32,2048]{1,0:T(8,128)(2,1)S(1)} %get-tuple-element.124), kind=kOutput, calls=%fused_computation.4.clone.1 | convolution fusion | flops 272629760 | bytes 459264 | tf_op jit(solution)/shard_map/while/body/eval_jaxpr/cr,rfb->fcb/dot_general | solution.py:52
  67.3 5.0 %fusion.12 = f32[16,8,32,256]{3,2,1,0:T(8,128)} fusion(f32[16,8,32,256]{3,2,1,0:T(8,128)} %get-tuple-element.112, s32[]{:T(128)} %get-tuple-element.111, s32[2048,8]{0,1:T(8,128)S(1)} %constant_dynamic-slice_fusion.2, bf16[32,2048]{1,0:T(8,128)(2,1)S(1)} %get-tuple-element.124), kind=kOutput, calls=%fused_computation.4.clone.1 | convolution fusion | flops 272629760 | bytes 459264 | tf_op jit(solution)/shard_map/while/body/eval_jaxpr/cr,rfb->fcb/dot_general | solution.py:52
  73.6 5.0 %fusion.12 = f32[16,8,32,256]{3,2,1,0:T(8,128)} fusion(f32[16,8,32,256]{3,2,1,0:T(8,128)} %get-tuple-element.112, s32[]{:T(128)} %get-tuple-element.111, s32[2048,8]{0,1:T(8,128)S(1)} %constant_dynamic-slice_fusion.2, bf16[32,2048]{1,0:T(8,128)(2,1)S(1)} %get-tuple-element.124), kind=kOutput, calls=%fused_computation.4.clone.1 | convolution fusion | flops 272629760 | bytes 459264 | tf_op jit(solution)/shard_map/while/body/eval_jaxpr/cr,rfb->fcb/dot_general | solution.py:52
  79.9 5.0 %fusion.12 = f32[16,8,32,256]{3,2,1,0:T(8,128)} fusion(f32[16,8,32,256]{3,2,1,0:T(8,128)} %get-tuple-element.112, s32[]{:T(128)} %get-tuple-element.111, s32[2048,8]{0,1:T(8,128)S(1)} %constant_dynamic-slice_fusion.2, bf16[32,2048]{1,0:T(8,128)(2,1)S(1)} %get-tuple-element.124), kind=kOutput, calls=%fused_computation.4.clone.1 | convolution fusion | flops 272629760 | bytes 459264 | tf_op jit(solution)/shard_map/while/body/eval_jaxpr/cr,rfb->fcb/dot_general | solution.py:52
  86.1 5.0 %fusion.12 = f32[16,8,32,256]{3,2,1,0:T(8,128)} fusion(f32[16,8,32,256]{3,2,1,0:T(8,128)} %get-tuple-element.112, s32[]{:T(128)} %get-tuple-element.111, s32[2048,8]{0,1:T(8,128)S(1)} %constant_dynamic-slice_fusion.2, bf16[32,2048]{1,0:T(8,128)(2,1)S(1)} %get-tuple-element.124), kind=kOutput, calls=%fused_computation.4.clone.1 | convolution fusion | flops 272629760 | bytes 459264 | tf_op jit(solution)/shard_map/while/body/eval_jaxpr/cr,rfb->fcb/dot_general | solution.py:52
  92.4 5.0 %fusion.12 = f32[16,8,32,256]{3,2,1,0:T(8,128)} fusion(f32[16,8,32,256]{3,2,1,0:T(8,128)} %get-tuple-element.112, s32[]{:T(128)} %get-tuple-element.111, s32[2048,8]{0,1:T(8,128)S(1)} %constant_dynamic-slice_fusion.2, bf16[32,2048]{1,0:T(8,128)(2,1)S(1)} %get-tuple-element.124), kind=kOutput, calls=%fused_computation.4.clone.1 | convolution fusion | flops 272629760 | bytes 459264 | tf_op jit(solution)/shard_map/while/body/eval_jaxpr/cr,rfb->fcb/dot_general | solution.py:52
  98.7 5.0 %fusion.12 = f32[16,8,32,256]{3,2,1,0:T(8,128)} fusion(f32[16,8,32,256]{3,2,1,0:T(8,128)} %get-tuple-element.112, s32[]{:T(128)} %get-tuple-element.111, s32[2048,8]{0,1:T(8,128)S(1)} %constant_dynamic-slice_fusion.2, bf16[32,2048]{1,0:T(8,128)(2,1)S(1)} %get-tuple-element.124), kind=kOutput, calls=%fused_computation.4.clone.1 | convolution fusion | flops 272629760 | bytes 459264 | tf_op jit(solution)/shard_map/while/body/eval_jaxpr/cr,rfb->fcb/dot_general | solution.py:52
  105.0 5.0 %fusion.12 = f32[16,8,32,256]{3,2,1,0:T(8,128)} fusion(f32[16,8,32,256]{3,2,1,0:T(8,128)} %get-tuple-element.112, s32[]{:T(128)} %get-tuple-element.111, s32[2048,8]{0,1:T(8,128)S(1)} %constant_dynamic-slice_fusion.2, bf16[32,2048]{1,0:T(8,128)(2,1)S(1)} %get-tuple-element.124), kind=kOutput, calls=%fused_computation.4.clone.1 | convolution fusion | flops 272629760 | bytes 459264 | tf_op jit(solution)/shard_map/while/body/eval_jaxpr/cr,rfb->fcb/dot_general | solution.py:52
  110.0 64.3 %reduce-scatter.4.cloned.1.call-done = f32[16,32,256]{2,1,0:T(8,128)} async-done(((f32[128,32,256]{2,1,0:T(8,128)}), f32[16,32,256]{2,1,0:T(8,128)}) %reduce-scatter.4.cloned.1.call-update) | async-done | bytes 524304 | tf_op jit(solution)/shard_map/reduce_scatter | solution.py:22
  174.4 35.9 %reduce-scatter.6.cloned.1.call-done = f32[2,32,256]{2,1,0:T(8,128)} async-done(((f32[16,32,256]{2,1,0:T(8,128)}), f32[2,32,256]{2,1,0:T(8,128)}) %reduce-scatter.6.cloned.1.call-update) | async-done | bytes 65552 | tf_op jit(solution)/shard_map/reduce_scatter | solution.py:22
  210.3 24.1 %reduce-scatter.8.cloned.1.call-done = f32[1,32,256]{2,1,0:T(8,128)} async-done(((f32[2,32,256]{2,1,0:T(8,128)}), f32[1,32,256]{2,1,0:T(8,128)}) %reduce-scatter.8.cloned.1.call-update) | async-done | bytes 32784 | tf_op jit(solution)/shard_map/reduce_scatter | solution.py:22
  234.4 0.8 reshape.55
  235.2 0.6 reduce-window.6
  236.5 0.8 fusion.8
  237.3 14.5 %pmax.35 = f32[16]{0:T(128)S(1)} all-reduce(f32[16]{0:T(128)S(1)} %get-tuple-element.67), channel_id=1, replica_groups=mesh['rows_0'=8,'rows_1'=8,'rows_2'=2,'feat_0'=2,'feat_1'=2] {'rows_0'}, use_global_device_ids=true, to_apply=%region_8.9 | all-reduce | flops 16 | bytes 128 | tf_op jit(solution)/shard_map/pmax | solution.py:27
  251.9 13.2 %pmax.36 = f32[16]{0:T(128)S(1)} all-reduce(f32[16]{0:T(128)S(1)} %pmax.35), channel_id=1, replica_groups=mesh['rows_0'=8,'rows_1'=8,'rows_2'=2,'feat_0'=2,'feat_1'=2] {'rows_1'}, use_global_device_ids=true, to_apply=%region_9.10 | all-reduce | flops 16 | bytes 128 | tf_op jit(solution)/shard_map/pmax | solution.py:27
  265.1 3.8 %pmax.37 = f32[16]{0:T(128)S(1)} all-reduce(f32[16]{0:T(128)S(1)} %pmax.36), channel_id=1, replica_groups=mesh['rows_0'=8,'rows_1'=8,'rows_2'=2,'feat_0'=2,'feat_1'=2] {'rows_2'}, use_global_device_ids=true, to_apply=%region_10.11 | all-reduce | flops 16 | bytes 128 | tf_op jit(solution)/shard_map/pmax | solution.py:27
  268.8 5.3 %pmax.38 = f32[16]{0:T(128)S(1)} all-reduce(f32[16]{0:T(128)S(1)} %pmax.37), channel_id=1, replica_groups=mesh['rows_0'=8,'rows_1'=8,'rows_2'=2,'feat_0'=2,'feat_1'=2] {'feat_0'}, use_global_device_ids=true, to_apply=%region_11.12 | all-reduce | flops 16 | bytes 128 | tf_op jit(solution)/shard_map/pmax | solution.py:27
  274.1 13.5 %pmax.39 = f32[16]{0:T(128)} all-reduce(f32[16]{0:T(128)S(1)} %pmax.38), channel_id=1, replica_groups=mesh['rows_0'=8,'rows_1'=8,'rows_2'=2,'feat_0'=2,'feat_1'=2] {'feat_1'}, use_global_device_ids=true, to_apply=%region_12.13 | all-reduce | flops 16 | bytes 128 | tf_op jit(solution)/shard_map/pmax | solution.py:27
  (49 shorter events, 9.2 us)
Async XLA Ops:
  7.2 167.2 %reduce-scatter.4.cloned.1.call-start = ((), (), s32[]{:S(2)}) async-start(), calls=%async_computation.3 | async-start | bytes 4718592 | tf_op jit(solution)/shard_map/reduce_scatter | solution.py:22
  110.0 100.3 %reduce-scatter.6.cloned.1.call-start = ((), (), s32[]{:S(2)}) async-start(), calls=%async_computation.4 | async-start | bytes 589824 | tf_op jit(solution)/shard_map/reduce_scatter | solution.py:22
  174.4 60.1 %reduce-scatter.8.cloned.1.call-start = ((), (), s32[]{:S(2)}) async-start(), calls=%async_computation.5 | async-start | bytes 98304 | tf_op jit(solution)/shard_map/reduce_scatter | solution.py:22
Sparse Core Ops, SparseCore 0:
  110.1 64.1 reduce-scatter.3
  177.1 33.1 reduce-scatter.5
  213.0 21.3 reduce-scatter.7
where the time goes:
time: 295 us; the launch traced here: 294 us
  waiting for transfers between devices  124 us (42%)
  matrix products  80.3 us (27%)
  blocking collectives  50.2 us (17%)
  between operations  13.8 us (5%)
  local copies, waits for them, and re-layouts  12.3 us (4%)
  loops' own time  10.6 us (4%)
    reduce_scatter x3, waiting for transfers between devices, own_rows(): total = lax.psum_scatter(total, axis, scatter_dimension=0, tiled=True)  124 us
    dot_general x16, matrix products, partial_hist(): jnp.einsum('cr,rfb->fcb', weights, onehot, preferred_element_type=jnp.flo...  80.3 us
    pmax x5, blocking collectives, one_axis_at_a_time(): return functools.reduce(lax.pmax, axes, array)  50.2 us
    another operation x1, loops' own time, body(): stacked = lax.map(one_group, jnp.arange(group_count, dtype=jnp.int32))  10.6 us
    dynamic_slice x16, local copies, waits for them, and re-layouts, body(): stacked = lax.map(one_group, jnp.arange(group_count, dtype=jnp.int32))  9.32 us
  transfers between devices with their start and end apart: 3, of which 3 were waited for; matrix products, arithmetic and copies ran while one was open for 0% of the time, Pallas kernels for 0%

commit v1 on v0

v1 whole, which is shorter than its diff:
```python
import jax
import jax.numpy as jnp
from jax import lax
from jax.experimental import pallas as pl
from jax.experimental.pallas import tpu as pltpu
from jax.sharding import Mesh
from jax.sharding import PartitionSpec as P

f32, bf16 = jnp.float32, jnp.bfloat16
MESH = pl.DeviceIdType.MESH
BITS = ("z2", "z1", "z0", "y2", "y1", "y0", "xl", "xh", "co")
ROWS, FEAT = BITS[:7], BITS[7:]
CUBE = ("z0", "y0", "xl")
RING = ("z2", "z1", "y2", "y1")
ROUNDS = (("co", "xh", "xl"), ("y2", "y1", "y0"), ("z2", "z1", "z0"))
MSG = 304
reg_lambda = 1.0


def subset(axes, index):
    return tuple(a for i, a in enumerate(axes) if index >> (len(axes) - 1 - i) & 1)


def peer(flips):
    return {a: 1 - lax.axis_index(a) for a in flips}


def column(flips):
    j = 0
    for a in ROWS:
        b = lax.axis_index(a)
        j = 2 * j + (1 - b if a in flips else b)
    return j


def row(ref, slot, r):
    return jnp.broadcast_to(ref[slot, r:r + 1, :], (16, 128)).astype(bf16)


def side(ref, slot, fs, qs, n, vals, row16):
    zero = jnp.zeros((), bf16)
    cols = []
    for k, q in enumerate(qs):
        rows = []
        for f in fs:
            key = row(ref, slot, f * 16 + q)
            masks = [key == row16 + bf16(16 * i) for i in range(n // 16)]
            for v in vals[k]:
                rows += [jnp.where(m, v, zero) for m in masks]
        cols.append(jnp.concatenate(rows, axis=0))
    return jnp.concatenate(cols, axis=1)


def prep_slot(slot, rbuf, lof, hif, metaf):
    leaf = rbuf[slot, 256:272, :].astype(f32)
    metaf[slot] = rbuf[slot, 272:304, :].astype(f32)
    for f in range(16):
        b = rbuf[slot, f * 16:(f + 1) * 16, :].astype(f32)
        w = 64.0 if f % 8 < 4 else 32.0
        hi = jnp.floor(b * (1.0 / w))
        lof[slot, f * 16:(f + 1) * 16, :] = b - w * hi
        hif[slot, f * 16:(f + 1) * 16, :] = hi * 16.0 + leaf


def tiles(slot, base, lof, hif, metaf, accs):
    row16 = lax.broadcasted_iota(jnp.int32, (16, 128), 0).astype(f32).astype(bf16)
    one = jnp.ones((), bf16)
    stage = [0, 0]

    def tile(mxu, acc, fs, qs, vals, a, b):
        fs = [base + f for f in fs]
        rhs = side(lof, slot, fs, qs, b, vals, row16)
        lhs = side(hif, slot, fs, qs, a, [[one], [one]], row16)
        pltpu.matmul_push_rhs(rhs, stage[mxu], mxu, transpose=True)
        pltpu.matmul_acc_lhs(acc, lhs, stage[mxu])
        stage[mxu] ^= 1

    for qp in range(8):
        qs = (2 * qp, 2 * qp + 1)
        vals = [[row(metaf, slot, q), row(metaf, slot, 16 + q)] for q in qs]
        tile(qp % 2, accs[2 + qp % 2], (4, 5, 6, 7), qs, vals, 128, 32)
        for fp in range(2):
            tile(fp, accs[fp], (2 * fp, 2 * fp + 1), qs, vals, 64, 64)


def pop_hists(accs, hs, base):
    for fp in range(2):
        r = pltpu.matmul_pop(accs[fp])
        hs[base + 2 * fp] = r[:64, :128]
        hs[base + 2 * fp + 1] = r[64:, 128:]
    both = pltpu.matmul_pop(accs[2]) + pltpu.matmul_pop(accs[3])
    for f in range(4):
        r = both[f * 128:(f + 1) * 128, f * 64:(f + 1) * 64]
        parts = []
        for h in range(4):
            e, o = r[32 * h:32 * h + 16], r[32 * h + 16:32 * h + 32]
            parts.append(jnp.concatenate([e[:, :32], o[:, :32], e[:, 32:], o[:, 32:]], axis=1))
        hs[base + 4 + f] = jnp.concatenate(parts, axis=0)


def prefix_over_lo(h, acc):
    r = lax.broadcasted_iota(jnp.int32, (256, 256), 0) & 127
    c = lax.broadcasted_iota(jnp.int32, (256, 256), 1)
    ones = jnp.where(((r < 64) & (c < 64) & (r <= c)) | ((r >= 64) & (c >= 64) & (c < 128) & (r <= c)), 1.0, 0.0).astype(bf16)
    h1 = h.astype(bf16)
    rest = h - h1.astype(f32)
    h2 = rest.astype(bf16)
    h3 = (rest - h2.astype(f32)).astype(bf16)
    pltpu.matmul_push_rhs(ones, 0, 0)
    pltpu.matmul_acc_lhs(acc, jnp.concatenate([h1, h2], axis=1), 0)
    pltpu.matmul_acc_lhs(acc, jnp.concatenate([h3, jnp.zeros_like(h3)], axis=1), None)
    return pltpu.matmul_pop(acc)[:, :128]


def left_sums(p):
    outs = []
    for v in range(2):
        offset = jnp.zeros((16, 1), f32)
        parts = []
        for hi in range(4):
            block = p[hi * 16:(hi + 1) * 16, v * 64:(v + 1) * 64]
            parts.append(block + offset)
            offset = offset + block[:, 63:64]
        outs.append(jnp.concatenate(parts, axis=1))
    return outs


def gain_of(left_grad, left_hess):
    total_grad = left_grad[:, 255:256]
    total_hess = left_hess[:, 255:256]
    right_grad = total_grad - left_grad
    right_hess = total_hess - left_hess
    return 0.5 * (
        left_grad * left_grad / (left_hess + reg_lambda)
        + right_grad * right_grad / (right_hess + reg_lambda)
        - total_grad * total_grad / (total_hess + reg_lambda)
    )


def kernel(bins, leaf, grad, hess, gains, best, tbuf, sbuf, rbuf, lof, hif, metaf, hs, rs, mine, theirs,
           row_send, row_recv, part_send, part_recv, max_send, max_recv):
    partners = {subset(CUBE, c) for c in range(1, 8)} | {subset(RING, e) for e in range(1, 16)}
    partners |= {subset(axes, m) for axes in ROUNDS for m in range(1, 8)}
    partners = sorted({tuple(sorted(p)) for p in partners})
    barrier = pltpu.get_barrier_semaphore()
    for p in partners:
        pl.semaphore_signal(barrier, inc=1, device_id=peer(p), device_id_type=MESH)

    for q in range(16):
        tbuf[pl.ds(q, 128, stride=16), :] = bins[q * 128:(q + 1) * 128, :].astype(f32).T
    meta = [leaf[...].astype(f32).astype(bf16), grad[...], hess[...]]

    def pack(c, store):
        for e in range(16):
            j = column(subset(CUBE, c) + subset(RING, e))
            store(e * 16, tbuf[pl.ds(pl.multiple_of(j * 16, 16), 16), :].astype(bf16))
        for i, m in enumerate(meta):
            store(256 + 16 * i, m)

    def to_sbuf(c):
        def store(r, v):
            sbuf[c, r:r + 16, :] = v
        return store

    def to_own(r, v):
        rbuf[0, r:r + 16, :] = v

    for c in range(7, 0, -1):
        pack(c, to_sbuf(c))

    def row_copy(c):
        return pltpu.make_async_remote_copy(
            src_ref=sbuf.at[c], dst_ref=rbuf.at[c], send_sem=row_send.at[c], recv_sem=row_recv.at[c],
            device_id=peer(subset(CUBE, c)), device_id_type=MESH)

    pl.semaphore_wait(barrier, len(partners))
    for c in range(7, 0, -1):
        row_copy(c).start()
    pack(0, to_own)

    def part_copy(e):
        return pltpu.make_async_remote_copy(
            src_ref=hs.at[e], dst_ref=rs.at[e], send_sem=part_send.at[e], recv_sem=part_recv.at[e],
            device_id=peer(subset(RING, e)), device_id_type=MESH)

    def scoped(*accs):
        prep_slot(0, rbuf, lof, hif, metaf)
        tiles(0, 8, lof, hif, metaf, accs)

        @pl.loop(1, 8)
        def _(s):
            pltpu.make_async_remote_copy(
                src_ref=sbuf.at[s], dst_ref=rbuf.at[s], send_sem=row_send.at[s], recv_sem=row_recv.at[s],
                device_id=peer(CUBE), device_id_type=MESH).wait_recv()
            prep_slot(s, rbuf, lof, hif, metaf)
            tiles(s, 8, lof, hif, metaf, accs)

        pop_hists(accs, hs, 8)
        for e in range(15, 7, -1):
            part_copy(e).start()

        @pl.loop(0, 8)
        def _(s):
            tiles(s, 0, lof, hif, metaf, accs)

        pop_hists(accs, hs, 0)
        for e in range(7, 0, -1):
            part_copy(e).start()

        total = hs[0]
        for e in range(15, 0, -1):
            part_copy(e).wait_recv()
            total = total + rs[e]
        left_grad, left_hess = left_sums(prefix_over_lo(total, accs[4]))
        gain = gain_of(left_grad, left_hess)
        gains[...] = gain
        top = jnp.broadcast_to(jnp.max(gain, axis=1, keepdims=True), (16, 128))
        sub = lax.broadcasted_iota(jnp.int32, (16, 128), 0)
        lane = lax.broadcasted_iota(jnp.int32, (16, 128), 1)
        here = jnp.max(jnp.where(sub == lane, top, -jnp.inf), axis=0, keepdims=True)
        for k, axes in enumerate(ROUNDS):
            mine[k] = here
            copies = [pltpu.make_async_remote_copy(
                src_ref=mine.at[k], dst_ref=theirs.at[8 * k + m], send_sem=max_send.at[8 * k + m], recv_sem=max_recv.at[8 * k + m],
                device_id=peer(subset(axes, m)), device_id_type=MESH) for m in range(1, 8)]
            for copy in copies:
                copy.start()
            for m, copy in enumerate(copies):
                copy.wait_recv()
                here = jnp.maximum(here, theirs[8 * k + m + 1])
            for copy in copies:
                copy.wait_send()
        best[...] = here

    pl.run_scoped(
        scoped, pltpu.ACC(0)((128, 256), f32), pltpu.ACC(1)((128, 256), f32), pltpu.ACC(0)((512, 256), f32),
        pltpu.ACC(1)((512, 256), f32), pltpu.ACC(0)((64, 256), f32))
    for c in range(1, 8):
        row_copy(c).wait_send()
    for e in range(1, 16):
        part_copy(e).wait_send()


def body(bin_index, leaf_ids, gradients, hessians):
    vmem = pl.BlockSpec(memory_space=pltpu.VMEM)
    gains, best = pl.pallas_call(
        kernel,
        out_shape=(jax.ShapeDtypeStruct((16, 256), f32), jax.ShapeDtypeStruct((1, 128), f32)),
        in_specs=[vmem] * 4,
        out_specs=(vmem, vmem),
        scratch_shapes=[
            pltpu.VMEM((2048, 128), f32),
            pltpu.VMEM((8, MSG, 128), bf16),
            pltpu.VMEM((8, MSG, 128), bf16),
            pltpu.VMEM((8, 256, 128), f32),
            pltpu.VMEM((8, 256, 128), f32),
            pltpu.VMEM((8, 32, 128), f32),
            pltpu.VMEM((16, 64, 128), f32),
            pltpu.VMEM((16, 64, 128), f32),
            pltpu.VMEM((3, 1, 128), f32),
            pltpu.VMEM((24, 1, 128), f32),
            pltpu.SemaphoreType.DMA((8,)),
            pltpu.SemaphoreType.DMA((8,)),
            pltpu.SemaphoreType.DMA((16,)),
            pltpu.SemaphoreType.DMA((16,)),
            pltpu.SemaphoreType.DMA((24,)),
            pltpu.SemaphoreType.DMA((24,)),
        ],
        compiler_params=pltpu.CompilerParams(collective_id=0, has_side_effects=True, vmem_limit_bytes=48 * 1024 * 1024),
    )(bin_index, leaf_ids.reshape(16, 128), gradients.reshape(16, 128), hessians.reshape(16, 128))
    return gains[None, None], best[0, :LEAVES]


LEAVES = 16


def solution(mesh):
    bits = Mesh(mesh.devices.reshape((2,) * 9), BITS)
    return jax.shard_map(
        body,
        mesh=bits,
        in_specs=(P(ROWS, FEAT), P(ROWS), P(ROWS), P(ROWS)),
        out_specs=(P(FEAT, ROWS, None, None), P()),
        check_vma=False,
    )
```

time: 295 us -> 66.6 us (0.23)
  waiting for transfers between devices: 124 us -> 0 us
  matrix products: 80.3 us -> 0 us
  Pallas kernels: 0 us -> 61.1 us
  blocking collectives: 50.2 us -> 0 us
  between operations: 13.8 us -> 0.65 us
  loops' own time: 10.6 us -> 0 us
  local copies, waits for them, and re-layouts: 12.3 us -> 4.4 us
    reduce_scatter x3 -> x0, waiting for transfers between devices: 124 us -> none  [own_rows(): total = lax.psum_scatter(total, axis, scatter_dimension=0, tiled=True)]
    dot_general x16 -> x0, matrix products: 80.3 us -> none  [partial_hist(): jnp.einsum('cr,rfb->fcb', weights, onehot, preferred_element_type=jnp.flo...]
    pallas_call x0 -> x1, Pallas kernels: none -> 61.1 us  [body(): pl.pallas_call(kernel, out_shape=(jax.ShapeDtypeStruct((16, 256), f32), j...]
    pmax x5 -> x0, blocking collectives: 50.2 us -> none  [one_axis_at_a_time(): return functools.reduce(lax.pmax, axes, array)]
    another operation x1 -> x0, loops' own time: 10.6 us -> none  [body(): stacked = lax.map(one_group, jnp.arange(group_count, dtype=jnp.int32))]
    dynamic_slice x32 -> x0, local copies, waits for them, and re-layouts: 9.5 us -> none  [the longest x16 9.32 us: body(): stacked = lax.map(one_group, jnp.arange(group_count, dtype=jnp.int32))]
    unnamed x0 -> x9, local copies, waits for them, and re-layouts: none -> 3.89 us
  transfers between devices with their start and end apart: 3 -> 0, of which waited for: 3 -> 0; matrix products, arithmetic and copies ran while one was open for 0% -> 0% of each run, Pallas kernels for 0% -> 0%
where the time goes in v1:
time: 66.6 us; the launch traced here: 66.2 us
  Pallas kernels  61.1 us (92%)
  local copies, waits for them, and re-layouts  4.4 us (7%)
    pallas_call x1, Pallas kernels, body(): pl.pallas_call(kernel, out_shape=(jax.ShapeDtypeStruct((16, 256), f32), j...  61.1 us
    unnamed x9, local copies, waits for them, and re-layouts  3.89 us

profile of v1, /device:TPU:1, one launch (start us, length us, event | category | flops | bytes accessed | tf_op | source)
XLA Modules:
  0.0 66.2 jit_solution(14741139595530334332)
XLA Ops:
  0.6 0.0 copy-start.2
  0.6 0.7 %copy-done.2 = bf16[2048]{0:T(1024)(128)(2,1)S(1)} copy-done((bf16[2048]{0:T(1024)(128)(2,1)S(1)}, bf16[2048]{0:T(1024)(128)(2,1)}, u32[]{:S(2)}) %copy-start.2) | copy-done | bytes 4120
  1.3 0.0 copy-start
  1.3 1.2 %copy-done = s32[2048,128]{1,0:T(8,128)S(1)} copy-done((s32[2048,128]{1,0:T(8,128)S(1)}, s32[2048,128]{1,0:T(8,128)}, u32[]{:S(2)}) %copy-start) | copy-done | bytes 1048600
  2.5 0.0 copy-start.1
  2.5 0.7 %copy-done.1 = s32[2048]{0:T(1024)S(1)} copy-done((s32[2048]{0:T(1024)S(1)}, s32[2048]{0:T(1024)}, u32[]{:S(2)}) %copy-start.1) | copy-done | bytes 8216
  3.2 0.0 copy-start.3
  3.2 0.7 %copy-done.3 = bf16[2048]{0:T(1024)(128)(2,1)S(1)} copy-done((bf16[2048]{0:T(1024)(128)(2,1)S(1)}, bf16[2048]{0:T(1024)(128)(2,1)}, u32[]{:S(2)}) %copy-start.3) | copy-done | bytes 4120
  3.9 61.1 %shard_map.59 = (f32[16,256]{1,0:T(8,128)S(1)}, f32[1,128]{1,0:T(1,128)S(1)}) custom-call(s32[2048,128]{1,0:T(8,128)S(1)} %copy-done, s32[16,128]{1,0:T(8,128)S(1)} %bitcast.7, bf16[16,128]{1,0:T(8,128)(2,1)S(1)} %bitcast.8, bf16[16,128]{1,0:T(8,128)(2,1)S(1)} %bitcast.9), custom_call_target="tpu_custom_call" | custom-call | tf_op jit(solution)/shard_map/pallas_call | solution.py:246
  65.1 0.5 slice_bitcast_fusion
  65.6 0.6 copy.7
Async XLA Ops:
  0.6 0.7 %copy-start.2 = (bf16[2048]{0:T(1024)(128)(2,1)S(1)}, bf16[2048]{0:T(1024)(128)(2,1)}, u32[]{:S(2)}) copy-start(bf16[2048]{0:T(1024)(128)(2,1)} %param.6) | copy-start | bytes 12292
  1.3 1.2 %copy-start = (s32[2048,128]{1,0:T(8,128)S(1)}, s32[2048,128]{1,0:T(8,128)}, u32[]{:S(2)}) copy-start(s32[2048,128]{1,0:T(8,128)} %bins.1) | copy-start | bytes 3145732
  2.5 0.7 %copy-start.1 = (s32[2048]{0:T(1024)S(1)}, s32[2048]{0:T(1024)}, u32[]{:S(2)}) copy-start(s32[2048]{0:T(1024)} %param.5) | copy-start | bytes 24580
  3.2 0.7 %copy-start.3 = (bf16[2048]{0:T(1024)(128)(2,1)S(1)}, bf16[2048]{0:T(1024)(128)(2,1)}, u32[]{:S(2)}) copy-start(bf16[2048]{0:T(1024)(128)(2,1)} %param.7) | copy-start | bytes 12292

commit v2 on v1

v2 whole, which is shorter than its diff:
```python
import jax
import jax.numpy as jnp
from jax import lax
from jax.experimental import pallas as pl
from jax.experimental.pallas import tpu as pltpu
from jax.sharding import Mesh
from jax.sharding import PartitionSpec as P

f32, bf16 = jnp.float32, jnp.bfloat16
MESH = pl.DeviceIdType.MESH
BITS = ("z2", "z1", "z0", "y2", "y1", "y0", "xl", "xh", "co")
ROWS, FEAT = BITS[:7], BITS[7:]
CUBE = ("z0", "y0", "xl")
RING = ("z2", "z1", "y2", "y1")
CUBES = [(), ("xl",), ("y0",), ("z0",), ("y0", "xl"), ("z0", "xl"), ("z0", "y0"), ("z0", "y0", "xl")]
PASSES = ((10, 15, 14, 11, 8, 2, 9, 6), (7, 13, 5, 12, 3, 4, 1, 0))
LINES = (("co", "xh", "xl"), ("y2", "y1", "y0"), ("z2", "z1", "z0"))
ROUNDS = (("z2", "z1", "z0", "co"), ("y2", "y1", "y0", "xh", "xl"))
FIRST = (0, 15)
META = 128
MSG = (176, 128)
reg_lambda = 1.0


def subset(axes, index):
    return tuple(a for i, a in enumerate(axes) if index >> (len(axes) - 1 - i) & 1)


def peer(flips):
    return {a: 1 - lax.axis_index(a) for a in flips}


def column(flips):
    j = 0
    for a in ROWS:
        b = lax.axis_index(a)
        j = 2 * j + (1 - b if a in flips else b)
    return j


def row(ref, slot, r):
    return jnp.broadcast_to(ref[slot, r:r + 1, :], (16, 128)).astype(bf16)


def side(ref, slot, fs, qs, n, vals, row16):
    zero = jnp.zeros((), bf16)
    cols = []
    for k, q in enumerate(qs):
        rows = []
        for f in fs:
            key = row(ref, slot, f * 16 + q)
            masks = [key == row16 + bf16(16 * i) for i in range(n // 16)]
            for v in vals[k]:
                rows += [jnp.where(m, v, zero) for m in masks]
        cols.append(jnp.concatenate(rows, axis=0))
    return jnp.concatenate(cols, axis=1)


def prep_meta(slot, rbuf, leaff, metaf):
    leaff[slot] = rbuf[slot, META:META + 16, :].astype(f32)
    metaf[slot] = rbuf[slot, META + 16:META + 48, :].astype(f32)


def prep_slot(g, slot, rbuf, lof, hif, leaff):
    leaf = leaff[slot]
    for f in range(8):
        b = rbuf[slot, f * 16:(f + 1) * 16, :].astype(f32)
        w = 64.0 if f < 4 else 32.0
        hi = jnp.floor(b * (1.0 / w))
        lof[slot, f * 16:(f + 1) * 16, :] = b - w * hi
        hif[slot, f * 16:(f + 1) * 16, :] = hi * 16.0 + leaf


def tiles(slot, lof, hif, metaf, accs):
    row16 = lax.broadcasted_iota(jnp.int32, (16, 128), 0).astype(f32).astype(bf16)
    one = jnp.ones((), bf16)
    stage = [0, 0]

    def tile(mxu, acc, fs, qs, vals, a, b):
        rhs = side(lof, slot, fs, qs, b, vals, row16)
        lhs = side(hif, slot, fs, qs, a, [[one], [one]], row16)
        pltpu.matmul_push_rhs(rhs, stage[mxu], mxu, transpose=True)
        pltpu.matmul_acc_lhs(acc, lhs, stage[mxu])
        stage[mxu] ^= 1

    for qp in range(8):
        qs = (2 * qp, 2 * qp + 1)
        vals = [[row(metaf, slot, q), row(metaf, slot, 16 + q)] for q in qs]
        tile(qp % 2, accs[2 + qp % 2], (4, 5, 6, 7), qs, vals, 128, 32)
        for fp in range(2):
            tile(fp, accs[fp], (2 * fp, 2 * fp + 1), qs, vals, 64, 64)


def pop_hists(accs, hs, es, more=False):
    def put(e, v):
        hs[e] = hs[e] + v if more else v

    for fp in range(2):
        r = pltpu.matmul_pop(accs[fp])
        put(es[2 * fp], r[:64, :128])
        put(es[2 * fp + 1], r[64:, 128:])
    both = pltpu.matmul_pop(accs[2]) + pltpu.matmul_pop(accs[3])
    for f in range(4):
        r = both[f * 128:(f + 1) * 128, f * 64:(f + 1) * 64]
        parts = []
        for h in range(4):
            e, o = r[32 * h:32 * h + 16], r[32 * h + 16:32 * h + 32]
            parts.append(jnp.concatenate([e[:, :32], o[:, :32], e[:, 32:], o[:, 32:]], axis=1))
        put(es[4 + f], jnp.concatenate(parts, axis=0))


def prefix_over_lo(h, acc):
    r = lax.broadcasted_iota(jnp.int32, (256, 256), 0) & 127
    c = lax.broadcasted_iota(jnp.int32, (256, 256), 1)
    ones = jnp.where(((r < 64) & (c < 64) & (r <= c)) | ((r >= 64) & (c >= 64) & (c < 128) & (r <= c)), 1.0, 0.0).astype(bf16)
    h1 = h.astype(bf16)
    rest = h - h1.astype(f32)
    h2 = rest.astype(bf16)
    h3 = (rest - h2.astype(f32)).astype(bf16)
    pltpu.matmul_push_rhs(ones, 0, 0)
    pltpu.matmul_acc_lhs(acc, jnp.concatenate([h1, h2], axis=1), 0)
    pltpu.matmul_acc_lhs(acc, jnp.concatenate([h3, jnp.zeros_like(h3)], axis=1), None)
    return pltpu.matmul_pop(acc)[:, :128]


def left_sums(p):
    outs = []
    for v in range(2):
        offset = jnp.zeros((16, 1), f32)
        parts = []
        for hi in range(4):
            block = p[hi * 16:(hi + 1) * 16, v * 64:(v + 1) * 64]
            parts.append(block + offset)
            offset = offset + block[:, 63:64]
        outs.append(jnp.concatenate(parts, axis=1))
    return outs


def gain_of(left_grad, left_hess):
    total_grad = left_grad[:, 255:256]
    total_hess = left_hess[:, 255:256]
    right_grad = total_grad - left_grad
    right_hess = total_hess - left_hess
    return 0.5 * (
        left_grad * left_grad / (left_hess + reg_lambda)
        + right_grad * right_grad / (right_hess + reg_lambda)
        - total_grad * total_grad / (total_hess + reg_lambda)
    )


def kernel(bins_hbm, leaf_hbm, grad_hbm, hess_hbm, gains, best, bins, leaf, grad, hess, tbuf, sbuf0, sbuf1, rbuf0, rbuf1,
           lof, hif, leaff, metaf, hs, rs, mine, theirs,
           in_sem, row_send, row_recv, part_send, part_recv, max_send, max_recv, relay_sem):
    loads = [pltpu.make_async_copy(bins_hbm.at[pl.ds(i * 1024, 1024)], bins.at[pl.ds(i * 1024, 1024)], in_sem.at[i]) for i in range(2)]
    loads += [pltpu.make_async_copy(a, b, in_sem.at[2 + i])
              for i, (a, b) in enumerate(((leaf_hbm, leaf), (grad_hbm, grad), (hess_hbm, hess)))]
    for load in loads:
        load.start()
    partners = set(CUBES[1:]) | {subset(axes, m) for axes in LINES for m in range(1, 8)}
    partners = sorted({tuple(sorted(p)) for p in partners})
    relays = [subset(("y2", "y1"), m) for m in range(1, 4)] + [("co",)] + [subset(("xh", "xl"), m) for m in range(1, 4)]
    barrier = pltpu.get_barrier_semaphore()
    for p in partners:
        pl.semaphore_signal(barrier, inc=1, device_id=peer(p), device_id_type=MESH)

    for q in range(16):
        if q % 8 == 0:
            loads[q // 8].wait()
        tbuf[pl.ds(q, 128, stride=16), :] = bins[q * 128:(q + 1) * 128, :].astype(f32).T
    for load in loads[2:]:
        load.wait()
    meta = [leaf[...].astype(f32).astype(bf16), grad[...], hess[...]]
    sbufs, rbufs = (sbuf0, sbuf1), (rbuf0, rbuf1)

    def pack(g, c):
        buf = sbufs[g] if c else rbufs[g]
        for i, e in enumerate(PASSES[g]):
            j = column(CUBES[c] + subset(RING, e))
            buf[c, i * 16:(i + 1) * 16, :] = tbuf[pl.ds(pl.multiple_of(j * 16, 16), 16), :].astype(bf16)
        if g == 0:
            for i, m in enumerate(meta):
                buf[c, META + 16 * i:META + 16 * (i + 1), :] = m

    def row_copy(g, c, flips):
        return pltpu.make_async_remote_copy(
            src_ref=sbufs[g].at[c], dst_ref=rbufs[g].at[c], send_sem=row_send.at[8 * g + c], recv_sem=row_recv.at[8 * g + c],
            device_id=peer(flips), device_id_type=MESH)

    for c in range(1, 8):
        pack(0, c)
    for g in (1, 0):
        pack(g, 0)
    def part_copy(e):
        return pltpu.make_async_remote_copy(
            src_ref=hs.at[e], dst_ref=rs.at[e], send_sem=part_send.at[e], recv_sem=part_recv.at[e],
            device_id=peer(subset(RING, e)), device_id_type=MESH)

    def scoped(*accs):
        prep_meta(0, rbuf0, leaff, metaf)
        prep_slot(1, 0, rbuf1, lof, hif, leaff)
        tiles(0, lof, hif, metaf, accs)
        pop_hists(accs, hs, PASSES[1])
        for c in range(1, 8):
            pack(1, c)
        pl.semaphore_wait(barrier, len(partners))
        for c in range(1, 8):
            row_copy(0, c, CUBES[c]).start()
        for p in relays:
            pl.semaphore_signal(relay_sem, inc=1, device_id=peer(p), device_id_type=MESH)
        prep_slot(0, 0, rbuf0, lof, hif, leaff)
        tiles(0, lof, hif, metaf, accs)

        def rest(g, lo, hi):
            @pl.loop(lo, hi)
            def _(s):
                row_copy(g, s, CUBE).wait_recv()
                if g == 0:
                    prep_meta(s, rbuf0, leaff, metaf)
                prep_slot(g, s, rbufs[g], lof, hif, leaff)
                tiles(s, lof, hif, metaf, accs)

        rest(0, 1, 4)
        for c in range(1, 8):
            row_copy(1, c, CUBES[c]).start()
        rest(0, 4, 8)
        for g in range(2):
            if g:
                rest(1, 1, 8)
            pop_hists(accs, hs, PASSES[g], more=g == 1)
            if g == 0:
                pl.semaphore_wait(relay_sem, len(relays))
            for e in PASSES[g]:
                if e:
                    part_copy(e).start()

        total = hs[0]
        for e in PASSES[0] + PASSES[1][:7]:
            part_copy(e).wait_recv()
            total = total + rs[e]
        left_grad, left_hess = left_sums(prefix_over_lo(total, accs[4]))
        gain = gain_of(left_grad, left_hess)
        gains[...] = gain
        top = jnp.broadcast_to(jnp.max(gain, axis=1, keepdims=True), (16, 128))
        sub = lax.broadcasted_iota(jnp.int32, (16, 128), 0)
        lane = lax.broadcasted_iota(jnp.int32, (16, 128), 1)
        here = jnp.max(jnp.where(sub == lane, top, -jnp.inf), axis=0, keepdims=True)
        sent = []
        for k, axes in enumerate(ROUNDS):
            mine[k] = here
            steps = range(1, 1 << len(axes))
            copies = [pltpu.make_async_remote_copy(
                src_ref=mine.at[k], dst_ref=theirs.at[FIRST[k] + m - 1], send_sem=max_send.at[FIRST[k] + m - 1],
                recv_sem=max_recv.at[FIRST[k] + m - 1], device_id=peer(subset(axes, m)), device_id_type=MESH) for m in steps]
            for copy in reversed(copies):
                copy.start()
            for copy in copies:
                copy.wait_recv()
            here = jnp.maximum(here, jnp.max(theirs[FIRST[k]:FIRST[k] + len(steps)], axis=0))
            sent += copies
        best[...] = here
        for copy in sent:
            copy.wait_send()

    pl.run_scoped(
        scoped, pltpu.ACC(0)((128, 256), f32), pltpu.ACC(1)((128, 256), f32), pltpu.ACC(0)((512, 256), f32),
        pltpu.ACC(1)((512, 256), f32), pltpu.ACC(0)((64, 256), f32))
    for g in range(2):
        for c in range(1, 8):
            row_copy(g, c, CUBES[c]).wait_send()
    for e in range(1, 16):
        part_copy(e).wait_send()


def body(bin_index, leaf_ids, gradients, hessians):
    vmem = pl.BlockSpec(memory_space=pltpu.VMEM)
    gains, best = pl.pallas_call(
        kernel,
        out_shape=(jax.ShapeDtypeStruct((16, 256), f32), jax.ShapeDtypeStruct((1, 128), f32)),
        in_specs=[pl.BlockSpec(memory_space=pltpu.HBM)] * 4,
        out_specs=(vmem, vmem),
        scratch_shapes=[
            pltpu.VMEM((2048, 128), jnp.int32),
            pltpu.VMEM((16, 128), jnp.int32),
            pltpu.VMEM((16, 128), bf16),
            pltpu.VMEM((16, 128), bf16),
            pltpu.VMEM((2048, 128), f32),
            pltpu.VMEM((8, MSG[0], 128), bf16),
            pltpu.VMEM((8, MSG[1], 128), bf16),
            pltpu.VMEM((8, MSG[0], 128), bf16),
            pltpu.VMEM((8, MSG[1], 128), bf16),
            pltpu.VMEM((8, 128, 128), f32),
            pltpu.VMEM((8, 128, 128), f32),
            pltpu.VMEM((8, 16, 128), f32),
            pltpu.VMEM((8, 32, 128), f32),
            pltpu.VMEM((16, 64, 128), f32),
            pltpu.VMEM((16, 64, 128), f32),
            pltpu.VMEM((2, 1, 128), f32),
            pltpu.VMEM((46, 1, 128), f32),
            pltpu.SemaphoreType.DMA((5,)),
            pltpu.SemaphoreType.DMA((16,)),
            pltpu.SemaphoreType.DMA((16,)),
            pltpu.SemaphoreType.DMA((16,)),
            pltpu.SemaphoreType.DMA((16,)),
            pltpu.SemaphoreType.DMA((46,)),
            pltpu.SemaphoreType.DMA((46,)),
            pltpu.SemaphoreType.REGULAR,
        ],
        compiler_params=pltpu.CompilerParams(collective_id=0, has_side_effects=True, vmem_limit_bytes=48 * 1024 * 1024),
    )(*(pltpu.with_memory_space_constraint(a, pltpu.HBM) for a in (
        bin_index, leaf_ids.reshape(16, 128), gradients.reshape(16, 128), hessians.reshape(16, 128))))
    return gains[None, None], best[0, :LEAVES]


LEAVES = 16


def solution(mesh):
    bits = Mesh(mesh.devices.reshape((2,) * 9), BITS)
    return jax.shard_map(
        body,
        mesh=bits,
        in_specs=(P(ROWS, FEAT), P(ROWS), P(ROWS), P(ROWS)),
        out_specs=(P(FEAT, ROWS, None, None), P()),
        check_vma=False,
    )
```

time: 66.6 us -> 56 us (0.84)
  Pallas kernels: 61.1 us -> 54.1 us
  local copies, waits for them, and re-layouts: 4.4 us -> 1.12 us
    pallas_call x1, Pallas kernels: 61.1 us -> 54.1 us  [body(): pl.pallas_call(kernel, out_shape=(jax.ShapeDtypeStruct((16, 256), f32), j...]
    unnamed x9 -> x1, local copies, waits for them, and re-layouts: 3.89 us -> 0.6 us
where the time goes in v2:
time: 56 us; the launch traced here: 55.9 us
  Pallas kernels  54.1 us (97%)
  local copies, waits for them, and re-layouts  1.12 us (2%)
  between operations  0.64 us (1%)
    pallas_call x1, Pallas kernels, body(): pl.pallas_call(kernel, out_shape=(jax.ShapeDtypeStruct((16, 256), f32), j...  54.1 us

profile of v2, /device:TPU:1, one launch (start us, length us, event | category | flops | bytes accessed | tf_op | source)
XLA Modules:
  0.0 55.9 jit_solution(4555780753468227270)
XLA Ops:
  0.6 54.1 %shard_map.59 = (f32[16,256]{1,0:T(8,128)S(1)}, f32[1,128]{1,0:T(1,128)S(1)}) custom-call(s32[2048,128]{1,0:T(8,128)} %bins_hbm.1, s32[16,128]{1,0:T(8,128)} %bitcast.7, bf16[16,128]{1,0:T(8,128)(2,1)} %bitcast.8, bf16[16,128]{1,0:T(8,128)(2,1)} %bitcast.9), custom_call_target="tpu_custom_call" | custom-call | tf_op jit(solution)/shard_map/pallas_call | solution.py:276
  54.7 0.5 slice_bitcast_fusion
  55.3 0.6 %copy.7 = f32[1,1,16,256]{3,2,1,0:T(8,128)} copy(f32[1,1,16,256]{3,2,1,0:T(8,128)S(1)} %bitcast.6) | data formatting | bytes 32768

commit v3 on v2

--- a/solution.py
+++ b/solution.py
@@ -11,7 +11,6 @@
 BITS = ("z2", "z1", "z0", "y2", "y1", "y0", "xl", "xh", "co")
 ROWS, FEAT = BITS[:7], BITS[7:]
 CUBE = ("z0", "y0", "xl")
-RING = ("z2", "z1", "y2", "y1")
 CUBES = [(), ("xl",), ("y0",), ("z0",), ("y0", "xl"), ("z0", "xl"), ("z0", "y0"), ("z0", "y0", "xl")]
 PASSES = ((10, 15, 14, 11, 8, 2, 9, 6), (7, 13, 5, 12, 3, 4, 1, 0))
 LINES = (("co", "xh", "xl"), ("y2", "y1", "y0"), ("z2", "z1", "z0"))
@@ -20,6 +19,11 @@
 META = 128
 MSG = (176, 128)
 reg_lambda = 1.0
+
+
+def ring(e):
+    z, y = (((), ("z1",), ("z2", "z0"), ("z2", "z1"))[e // 4], ((), ("y1",), ("y2", "y0"), ("y2", "y1"))[e % 4])
+    return z + y
 
 
 def subset(axes, index):
@@ -113,11 +117,11 @@
     r = lax.broadcasted_iota(jnp.int32, (256, 256), 0) & 127
     c = lax.broadcasted_iota(jnp.int32, (256, 256), 1)
     ones = jnp.where(((r < 64) & (c < 64) & (r <= c)) | ((r >= 64) & (c >= 64) & (c < 128) & (r <= c)), 1.0, 0.0).astype(bf16)
+    pltpu.matmul_push_rhs(ones, 0, 0)
     h1 = h.astype(bf16)
     rest = h - h1.astype(f32)
     h2 = rest.astype(bf16)
     h3 = (rest - h2.astype(f32)).astype(bf16)
-    pltpu.matmul_push_rhs(ones, 0, 0)
     pltpu.matmul_acc_lhs(acc, jnp.concatenate([h1, h2], axis=1), 0)
     pltpu.matmul_acc_lhs(acc, jnp.concatenate([h3, jnp.zeros_like(h3)], axis=1), None)
     return pltpu.matmul_pop(acc)[:, :128]
@@ -158,7 +162,7 @@
         load.start()
     partners = set(CUBES[1:]) | {subset(axes, m) for axes in LINES for m in range(1, 8)}
     partners = sorted({tuple(sorted(p)) for p in partners})
-    relays = [subset(("y2", "y1"), m) for m in range(1, 4)] + [("co",)] + [subset(("xh", "xl"), m) for m in range(1, 4)]
+    relays = [ring(e) for e in range(1, 4)] + [("co",)] + [subset(("xh", "xl"), m) for m in range(1, 4)]
     barrier = pltpu.get_barrier_semaphore()
     for p in partners:
         pl.semaphore_signal(barrier, inc=1, device_id=peer(p), device_id_type=MESH)
@@ -175,7 +179,7 @@
     def pack(g, c):
         buf = sbufs[g] if c else rbufs[g]
         for i, e in enumerate(PASSES[g]):
-            j = column(CUBES[c] + subset(RING, e))
+            j = column(set(CUBES[c]) ^ set(ring(e)))
             buf[c, i * 16:(i + 1) * 16, :] = tbuf[pl.ds(pl.multiple_of(j * 16, 16), 16), :].astype(bf16)
         if g == 0:
             for i, m in enumerate(meta):
@@ -193,39 +197,41 @@
     def part_copy(e):
         return pltpu.make_async_remote_copy(
             src_ref=hs.at[e], dst_ref=rs.at[e], send_sem=part_send.at[e], recv_sem=part_recv.at[e],
-            device_id=peer(subset(RING, e)), device_id_type=MESH)
+            device_id=peer(ring(e)), device_id_type=MESH)
 
     def scoped(*accs):
         prep_meta(0, rbuf0, leaff, metaf)
+        pl.semaphore_wait(barrier, len(partners))
+        for c in range(1, 8):
+            row_copy(0, c, CUBES[c]).start()
+        for p in relays:
+            pl.semaphore_signal(relay_sem, inc=1, device_id=peer(p), device_id_type=MESH)
         prep_slot(1, 0, rbuf1, lof, hif, leaff)
         tiles(0, lof, hif, metaf, accs)
         pop_hists(accs, hs, PASSES[1])
         for c in range(1, 8):
             pack(1, c)
-        pl.semaphore_wait(barrier, len(partners))
-        for c in range(1, 8):
-            row_copy(0, c, CUBES[c]).start()
-        for p in relays:
-            pl.semaphore_signal(relay_sem, inc=1, device_id=peer(p), device_id_type=MESH)
         prep_slot(0, 0, rbuf0, lof, hif, leaff)
         tiles(0, lof, hif, metaf, accs)
 
-        def rest(g, lo, hi):
-            @pl.loop(lo, hi)
-            def _(s):
-                row_copy(g, s, CUBE).wait_recv()
+        def rest(g, slots):
+            for c in slots:
+                row_copy(g, c, CUBES[c]).wait_recv()
+            for c in slots:
                 if g == 0:
-                    prep_meta(s, rbuf0, leaff, metaf)
-                prep_slot(g, s, rbufs[g], lof, hif, leaff)
-                tiles(s, lof, hif, metaf, accs)
-
-        rest(0, 1, 4)
+                    prep_meta(c, rbuf0, leaff, metaf)
+                prep_slot(g, c, rbufs[g], lof, hif, leaff)
+            for c in slots:
+                tiles(c, lof, hif, metaf, accs)
+
         for c in range(1, 8):
             row_copy(1, c, CUBES[c]).start()
-        rest(0, 4, 8)
+        rest(0, range(1, 4))
+        rest(0, range(4, 8))
         for g in range(2):
             if g:
-                rest(1, 1, 8)
+                rest(1, range(1, 4))
+                rest(1, range(4, 8))
             pop_hists(accs, hs, PASSES[g], more=g == 1)
             if g == 0:
                 pl.semaphore_wait(relay_sem, len(relays))

time: 56 us -> 52.8 us (0.943)
  Pallas kernels: 54.1 us -> 50.9 us
    pallas_call x1, Pallas kernels: 54.1 us -> 50.9 us  [body(): pl.pallas_call(kernel, out_shape=(jax.ShapeDtypeStruct((16, 256), f32), j...]
where the time goes in v3:
time: 52.8 us; the launch traced here: 52.7 us
  Pallas kernels  50.9 us (96%)
  local copies, waits for them, and re-layouts  1.12 us (2%)
  between operations  0.64 us (1%)
    pallas_call x1, Pallas kernels, body(): pl.pallas_call(kernel, out_shape=(jax.ShapeDtypeStruct((16, 256), f32), j...  50.9 us

profile of v3, /device:TPU:1, one launch (start us, length us, event | category | flops | bytes accessed | tf_op | source)
XLA Modules:
  0.0 52.7 jit_solution(10668496016456668667)
XLA Ops:
  0.6 50.9 %shard_map.59 = (f32[16,256]{1,0:T(8,128)S(1)}, f32[1,128]{1,0:T(1,128)S(1)}) custom-call(s32[2048,128]{1,0:T(8,128)} %bins_hbm.1, s32[16,128]{1,0:T(8,128)} %bitcast.7, bf16[16,128]{1,0:T(8,128)(2,1)} %bitcast.8, bf16[16,128]{1,0:T(8,128)(2,1)} %bitcast.9), custom_call_target="tpu_custom_call" | custom-call | tf_op jit(solution)/shard_map/pallas_call | solution.py:282
  51.5 0.5 slice_bitcast_fusion
  52.1 0.6 %copy.7 = f32[1,1,16,256]{3,2,1,0:T(8,128)} copy(f32[1,1,16,256]{3,2,1,0:T(8,128)S(1)} %bitcast.6) | data formatting | bytes 32768

commit v4 on v3

--- a/solution.py
+++ b/solution.py
@@ -95,9 +95,24 @@
             tile(fp, accs[fp], (2 * fp, 2 * fp + 1), qs, vals, 64, 64)
 
 
-def pop_hists(accs, hs, es, more=False):
+def halves(v, side):
+    part = v[:, side * 64:(side + 1) * 64]
+    return jnp.concatenate([part[:32], part[32:]], axis=1)
+
+
+def pop_hists(accs, hs, es, hg, hb, hold=False, more=False):
     def put(e, v):
-        hs[e] = hs[e] + v if more else v
+        if more:
+            v = hs[e] + v
+        if hold:
+            hs[e] = v
+            return
+        hg[e] = halves(v, 0)
+        h = halves(v, 1)
+        if e:
+            hb[e] = h.astype(bf16)
+        else:
+            hs[0, 0:32, :] = h
 
     for fp in range(2):
         r = pltpu.matmul_pop(accs[fp])
@@ -153,7 +168,7 @@
 
 
 def kernel(bins_hbm, leaf_hbm, grad_hbm, hess_hbm, gains, best, bins, leaf, grad, hess, tbuf, sbuf0, sbuf1, rbuf0, rbuf1,
-           lof, hif, leaff, metaf, hs, rs, mine, theirs,
+           lof, hif, leaff, metaf, hs, hg, hb, rg, rb, mine, theirs,
            in_sem, row_send, row_recv, part_send, part_recv, max_send, max_recv, relay_sem):
     loads = [pltpu.make_async_copy(bins_hbm.at[pl.ds(i * 1024, 1024)], bins.at[pl.ds(i * 1024, 1024)], in_sem.at[i]) for i in range(2)]
     loads += [pltpu.make_async_copy(a, b, in_sem.at[2 + i])
@@ -194,10 +209,10 @@
         pack(0, c)
     for g in (1, 0):
         pack(g, 0)
-    def part_copy(e):
-        return pltpu.make_async_remote_copy(
-            src_ref=hs.at[e], dst_ref=rs.at[e], send_sem=part_send.at[e], recv_sem=part_recv.at[e],
-            device_id=peer(ring(e)), device_id_type=MESH)
+    def part_copies(e):
+        return [pltpu.make_async_remote_copy(
+            src_ref=src.at[e], dst_ref=dst.at[e], send_sem=part_send.at[i, e], recv_sem=part_recv.at[i, e],
+            device_id=peer(ring(e)), device_id_type=MESH) for i, (src, dst) in enumerate(((hg, rg), (hb, rb)))]
 
     def scoped(*accs):
         prep_meta(0, rbuf0, leaff, metaf)
@@ -208,7 +223,7 @@
             pl.semaphore_signal(relay_sem, inc=1, device_id=peer(p), device_id_type=MESH)
         prep_slot(1, 0, rbuf1, lof, hif, leaff)
         tiles(0, lof, hif, metaf, accs)
-        pop_hists(accs, hs, PASSES[1])
+        pop_hists(accs, hs, PASSES[1], hg, hb, hold=True)
         for c in range(1, 8):
             pack(1, c)
         prep_slot(0, 0, rbuf0, lof, hif, leaff)
@@ -232,17 +247,22 @@
             if g:
                 rest(1, range(1, 4))
                 rest(1, range(4, 8))
-            pop_hists(accs, hs, PASSES[g], more=g == 1)
+            pop_hists(accs, hs, PASSES[g], hg, hb, more=g == 1)
             if g == 0:
                 pl.semaphore_wait(relay_sem, len(relays))
             for e in PASSES[g]:
                 if e:
-                    part_copy(e).start()
-
-        total = hs[0]
+                    for copy in part_copies(e):
+                        copy.start()
+
+        g_sum, h_sum = hg[0], hs[0, 0:32, :]
         for e in PASSES[0] + PASSES[1][:7]:
-            part_copy(e).wait_recv()
-            total = total + rs[e]
+            for copy in part_copies(e):
+                copy.wait_recv()
+            g_sum = g_sum + rg[e]
+            h_sum = h_sum + rb[e].astype(f32)
+        total = jnp.concatenate([
+            jnp.concatenate([g_sum[:, :64], h_sum[:, :64]], axis=1), jnp.concatenate([g_sum[:, 64:], h_sum[:, 64:]], axis=1)], axis=0)
         left_grad, left_hess = left_sums(prefix_over_lo(total, accs[4]))
         gain = gain_of(left_grad, left_hess)
         gains[...] = gain
@@ -274,7 +294,8 @@
         for c in range(1, 8):
             row_copy(g, c, CUBES[c]).wait_send()
     for e in range(1, 16):
-        part_copy(e).wait_send()
+        for copy in part_copies(e):
+            copy.wait_send()
 
 
 def body(bin_index, leaf_ids, gradients, hessians):
@@ -299,14 +320,17 @@
             pltpu.VMEM((8, 16, 128), f32),
             pltpu.VMEM((8, 32, 128), f32),
             pltpu.VMEM((16, 64, 128), f32),
-            pltpu.VMEM((16, 64, 128), f32),
+            pltpu.VMEM((16, 32, 128), f32),
+            pltpu.VMEM((16, 32, 128), bf16),
+            pltpu.VMEM((16, 32, 128), f32),
+            pltpu.VMEM((16, 32, 128), bf16),
             pltpu.VMEM((2, 1, 128), f32),
             pltpu.VMEM((46, 1, 128), f32),
             pltpu.SemaphoreType.DMA((5,)),
             pltpu.SemaphoreType.DMA((16,)),
             pltpu.SemaphoreType.DMA((16,)),
-            pltpu.SemaphoreType.DMA((16,)),
-            pltpu.SemaphoreType.DMA((16,)),
+            pltpu.SemaphoreType.DMA((2, 16)),
+            pltpu.SemaphoreType.DMA((2, 16)),
             pltpu.SemaphoreType.DMA((46,)),
             pltpu.SemaphoreType.DMA((46,)),
             pltpu.SemaphoreType.REGULAR,

time: 52.8 us -> 52.3 us (level)
    pallas_call x1, Pallas kernels: 50.9 us -> 50.4 us  [body(): pl.pallas_call(kernel, out_shape=(jax.ShapeDtypeStruct((16, 256), f32), j...]
where the time goes in v4:
time: 52.3 us; the launch traced here: 52.1 us
  Pallas kernels  50.4 us (96%)
  local copies, waits for them, and re-layouts  1.12 us (2%)
  between operations  0.64 us (1%)
    pallas_call x1, Pallas kernels, body(): pl.pallas_call(kernel, out_shape=(jax.ShapeDtypeStruct((16, 256), f32), j...  50.4 us

profile of v4, /device:TPU:1, one launch (start us, length us, event | category | flops | bytes accessed | tf_op | source)
XLA Modules:
  0.0 52.1 jit_solution(528924940406111131)
XLA Ops:
  0.6 50.4 %shard_map.59 = (f32[16,256]{1,0:T(8,128)S(1)}, f32[1,128]{1,0:T(1,128)S(1)}) custom-call(s32[2048,128]{1,0:T(8,128)} %bins_hbm.1, s32[16,128]{1,0:T(8,128)} %bitcast.7, bf16[16,128]{1,0:T(8,128)(2,1)} %bitcast.8, bf16[16,128]{1,0:T(8,128)(2,1)} %bitcast.9), custom_call_target="tpu_custom_call" | custom-call | tf_op jit(solution)/shard_map/pallas_call | solution.py:303
  51.0 0.5 slice_bitcast_fusion
  51.5 0.6 %copy.7 = f32[1,1,16,256]{3,2,1,0:T(8,128)} copy(f32[1,1,16,256]{3,2,1,0:T(8,128)S(1)} %bitcast.6) | data formatting | bytes 32768

commit v5 on v3

--- a/solution.py
+++ b/solution.py
@@ -12,7 +12,7 @@
 ROWS, FEAT = BITS[:7], BITS[7:]
 CUBE = ("z0", "y0", "xl")
 CUBES = [(), ("xl",), ("y0",), ("z0",), ("y0", "xl"), ("z0", "xl"), ("z0", "y0"), ("z0", "y0", "xl")]
-PASSES = ((10, 15, 14, 11, 8, 2, 9, 6), (7, 13, 5, 12, 3, 4, 1, 0))
+PASSES = ((10, 14, 11, 15, 9, 6, 13, 7), (5, 8, 2, 12, 3, 4, 1, 0))
 LINES = (("co", "xh", "xl"), ("y2", "y1", "y0"), ("z2", "z1", "z0"))
 ROUNDS = (("z2", "z1", "z0", "co"), ("y2", "y1", "y0", "xh", "xl"))
 FIRST = (0, 15)
@@ -32,6 +32,11 @@
 
 def peer(flips):
     return {a: 1 - lax.axis_index(a) for a in flips}
+
+
+def hops(flips):
+    far = {"y2": 4, "y1": 2, "y0": 1, "z2": 4, "z1": 2, "z0": 1, "xh": 2, "xl": 1, "co": 1}
+    return sum(far[a] for a in flips if not (a[0] + "2" in flips and a[1] == "1" or a == "xl" and "xh" in flips))
 
 
 def column(flips):
@@ -257,8 +262,8 @@
             copies = [pltpu.make_async_remote_copy(
                 src_ref=mine.at[k], dst_ref=theirs.at[FIRST[k] + m - 1], send_sem=max_send.at[FIRST[k] + m - 1],
                 recv_sem=max_recv.at[FIRST[k] + m - 1], device_id=peer(subset(axes, m)), device_id_type=MESH) for m in steps]
-            for copy in reversed(copies):
-                copy.start()
+            for m in sorted(steps, key=lambda m: -hops(subset(axes, m))):
+                copies[m - 1].start()
             for copy in copies:
                 copy.wait_recv()
             here = jnp.maximum(here, jnp.max(theirs[FIRST[k]:FIRST[k] + len(steps)], axis=0))

time: 52.8 us -> 53.6 us (1.015)
  Pallas kernels: 50.9 us -> 51.7 us
    pallas_call x1, Pallas kernels: 50.9 us -> 51.7 us  [body(): pl.pallas_call(kernel, out_shape=(jax.ShapeDtypeStruct((16, 256), f32), j...]
where the time goes in v5:
time: 53.6 us; the launch traced here: 53.5 us
  Pallas kernels  51.7 us (96%)
  local copies, waits for them, and re-layouts  1.12 us (2%)
  between operations  0.64 us (1%)
    pallas_call x1, Pallas kernels, body(): pl.pallas_call(kernel, out_shape=(jax.ShapeDtypeStruct((16, 256), f32), j...  51.7 us

profile of v5, /device:TPU:1, one launch (start us, length us, event | category | flops | bytes accessed | tf_op | source)
XLA Modules:
  0.0 53.5 jit_solution(11622961285134428177)
XLA Ops:
  0.6 51.7 %shard_map.59 = (f32[16,256]{1,0:T(8,128)S(1)}, f32[1,128]{1,0:T(1,128)S(1)}) custom-call(s32[2048,128]{1,0:T(8,128)} %bins_hbm.1, s32[16,128]{1,0:T(8,128)} %bitcast.7, bf16[16,128]{1,0:T(8,128)(2,1)} %bitcast.8, bf16[16,128]{1,0:T(8,128)(2,1)} %bitcast.9), custom_call_target="tpu_custom_call" | custom-call | tf_op jit(solution)/shard_map/pallas_call | solution.py:287
  52.4 0.5 slice_bitcast_fusion
  52.9 0.6 %copy.7 = f32[1,1,16,256]{3,2,1,0:T(8,128)} copy(f32[1,1,16,256]{3,2,1,0:T(8,128)S(1)} %bitcast.6) | data formatting | bytes 32768

commit v6 on v3

--- a/solution.py
+++ b/solution.py
@@ -34,6 +34,11 @@
     return {a: 1 - lax.axis_index(a) for a in flips}
 
 
+def hops(flips):
+    far = {"y2": 4, "y1": 2, "y0": 1, "z2": 4, "z1": 2, "z0": 1, "xh": 2, "xl": 1, "co": 1}
+    return sum(far[a] for a in flips if not (a[0] + "2" in flips and a[1] == "1" or a == "xl" and "xh" in flips))
+
+
 def column(flips):
     j = 0
     for a in ROWS:
@@ -161,7 +166,7 @@
     for load in loads:
         load.start()
     partners = set(CUBES[1:]) | {subset(axes, m) for axes in LINES for m in range(1, 8)}
-    partners = sorted({tuple(sorted(p)) for p in partners})
+    partners = sorted({tuple(sorted(p)) for p in partners}, key=lambda p: (-hops(p), p))
     relays = [ring(e) for e in range(1, 4)] + [("co",)] + [subset(("xh", "xl"), m) for m in range(1, 4)]
     barrier = pltpu.get_barrier_semaphore()
     for p in partners:
@@ -214,9 +219,11 @@
         prep_slot(0, 0, rbuf0, lof, hif, leaff)
         tiles(0, lof, hif, metaf, accs)
 
-        def rest(g, slots):
+        def rest(g, slots, then=()):
             for c in slots:
                 row_copy(g, c, CUBES[c]).wait_recv()
+            for c in then:
+                row_copy(1, c, CUBES[c]).start()
             for c in slots:
                 if g == 0:
                     prep_meta(c, rbuf0, leaff, metaf)
@@ -224,9 +231,7 @@
             for c in slots:
                 tiles(c, lof, hif, metaf, accs)
 
-        for c in range(1, 8):
-            row_copy(1, c, CUBES[c]).start()
-        rest(0, range(1, 4))
+        rest(0, range(1, 4), then=range(1, 8))
         rest(0, range(4, 8))
         for g in range(2):
             if g:

time: 52.8 us -> 53 us (level)
  no operation moved by 1% of the time
where the time goes in v6:
time: 53 us; the launch traced here: 52.8 us
  Pallas kernels  51.1 us (96%)
  local copies, waits for them, and re-layouts  1.12 us (2%)
  between operations  0.64 us (1%)
    pallas_call x1, Pallas kernels, body(): pl.pallas_call(kernel, out_shape=(jax.ShapeDtypeStruct((16, 256), f32), j...  51.1 us

profile of v6, /device:TPU:1, one launch (start us, length us, event | category | flops | bytes accessed | tf_op | source)
XLA Modules:
  0.0 52.8 jit_solution(5756046385538457014)
XLA Ops:
  0.6 51.1 %shard_map.59 = (f32[16,256]{1,0:T(8,128)S(1)}, f32[1,128]{1,0:T(1,128)S(1)}) custom-call(s32[2048,128]{1,0:T(8,128)} %bins_hbm.1, s32[16,128]{1,0:T(8,128)} %bitcast.7, bf16[16,128]{1,0:T(8,128)(2,1)} %bitcast.8, bf16[16,128]{1,0:T(8,128)(2,1)} %bitcast.9), custom_call_target="tpu_custom_call" | custom-call | tf_op jit(solution)/shard_map/pallas_call | solution.py:287
  51.7 0.5 slice_bitcast_fusion
  52.2 0.6 %copy.7 = f32[1,1,16,256]{3,2,1,0:T(8,128)} copy(f32[1,1,16,256]{3,2,1,0:T(8,128)S(1)} %bitcast.6) | data formatting | bytes 32768
